TPU v7x, 8 devices: a whole 2x2x1 slice. The times are simulated.
8 devices in a mesh: data: 1 (over z), dap: 8 (over y, x, core).
Axes of the slice: x: 2, y: 2, z: 1, core: 2. Of those that a mesh axis runs over, the one named last changes fastest.
Arguments:
- pair_act: bfloat16 [768, 768, 128], P(('data', 'dap'))
- pair_mask: int32 [768, 768], P(('data', 'dap'))
- d_pair_out: bfloat16 [768, 768, 128], P(('data', 'dap'))
- ln_pair: bfloat16 [2, 2, 128], replicated
- w_proj: bfloat16 [2, 128, 512], replicated
- w_gate: bfloat16 [2, 128, 128], replicated
- ln_chan: bfloat16 [2, 2, 128], replicated
- w_out: bfloat16 [2, 128, 128], replicated
Outputs:
- output 1: bfloat16 [768, 768, 128], P(('data', 'dap'))
- output 2: bfloat16 [768, 768, 128], P(('data', 'dap'))
- output 3: bfloat16 [2, 2, 128], P('data')
- output 4: bfloat16 [2, 128, 512], P('data')
- output 5: bfloat16 [2, 128, 128], P('data')
- output 6: bfloat16 [2, 2, 128], P('data')
- output 7: bfloat16 [2, 128, 128], P('data')
All inputs are finite; a program needn't handle non-finite values.
Results may differ from a plain program's by a relative error of at most 0.0133311.
Values are sent between devices in bfloat16 or wider.
A program may use at most 1 GiB of HBM per device.

v0:
```python
import jax
import jax.numpy as jnp
from jax import lax
from jax.sharding import PartitionSpec as P

LN_EPS = 1e-5
GROUP_AXIS = 'dap'


def layer_norm(values, gain_vec, shift_vec, norm_axis):
    mean_val = jnp.mean(values, axis=norm_axis, keepdims=True)
    centered = values - mean_val
    variance = jnp.mean(centered * centered, axis=norm_axis, keepdims=True)
    return centered * lax.rsqrt(variance + LN_EPS) * gain_vec + shift_vec


def norm_pair(values, ln_params):
    return layer_norm(values, ln_params[0], ln_params[1], -1)


def norm_chan(values, ln_params):
    return layer_norm(values, ln_params[0][:, None, None], ln_params[1][:, None, None], 0)


def to_channels(row_blocks):
    chan_dim = row_blocks.ndim - 3
    return lax.all_to_all(row_blocks, GROUP_AXIS, chan_dim, chan_dim + 1, tiled=True)


def to_rows(chan_blocks):
    chan_dim = chan_blocks.ndim - 3
    return lax.all_to_all(chan_blocks, GROUP_AXIS, chan_dim + 1, chan_dim, tiled=True)


def update_forward(z_rows, mask_f, ln_p, w_proj, w_gate, ln_q, w_out, incoming):
    z_float = z_rows.astype(jnp.float32)
    x_float, pair_back = jax.vjp(norm_pair, z_float, ln_p.astype(jnp.float32))
    x_norm = x_float.astype(jnp.bfloat16)
    proj_all = jnp.einsum('ijd,de->eij', x_norm, w_proj, preferred_element_type=jnp.float32)
    gate_val = jax.nn.sigmoid(jnp.einsum('ijd,de->ije', x_norm, w_gate, preferred_element_type=jnp.float32))
    lin_a, pre_ga, lin_b, pre_gb = jnp.split(proj_all, 4, axis=0)
    sig_a = jax.nn.sigmoid(pre_ga)
    sig_b = jax.nn.sigmoid(pre_gb)
    left_proj = (mask_f * sig_a * lin_a).astype(jnp.bfloat16)
    right_proj = (mask_f * sig_b * lin_b).astype(jnp.bfloat16)
    chan_pair = to_channels(jnp.stack([left_proj, right_proj]))
    if incoming:
        tri_prod = jnp.einsum('cki,ckj->cij', chan_pair[0], chan_pair[1], preferred_element_type=jnp.float32)
    else:
        tri_prod = jnp.einsum('cik,cjk->cij', chan_pair[0], chan_pair[1], preferred_element_type=jnp.float32)
    t_rows = to_rows(tri_prod.astype(jnp.bfloat16))
    y_float, chan_back = jax.vjp(norm_chan, t_rows.astype(jnp.float32), ln_q.astype(jnp.float32))
    y_norm = y_float.astype(jnp.bfloat16)
    update_f = jnp.einsum('cij,cd->ijd', y_norm, w_out, preferred_element_type=jnp.float32)
    z_new = (z_float + gate_val * update_f).astype(jnp.bfloat16)
    saved_fwd = dict(pair_back=pair_back, chan_back=chan_back, x_norm=x_norm, lin_a=lin_a, sig_a=sig_a, lin_b=lin_b, sig_b=sig_b, chan_pair=chan_pair, y_norm=y_norm, update_f=update_f, gate_val=gate_val)
    return z_new, saved_fwd


def update_backward(d_new, saved_fwd, mask_f, w_proj, w_gate, w_out, incoming):
    d_newf = d_new.astype(jnp.float32)
    gate_val = saved_fwd['gate_val']
    d_gate = (d_newf * saved_fwd['update_f'] * gate_val * (1.0 - gate_val)).astype(jnp.bfloat16)
    d_update = (d_newf * gate_val).astype(jnp.bfloat16)
    g_w_out = jnp.einsum('cij,ijd->cd', saved_fwd['y_norm'], d_update, preferred_element_type=jnp.float32)
    d_y = jnp.einsum('ijd,cd->cij', d_update, w_out, preferred_element_type=jnp.float32).astype(jnp.bfloat16)
    d_t, g_ln_q = saved_fwd['chan_back'](d_y.astype(jnp.float32))
    d_chan = to_channels(d_t.astype(jnp.bfloat16))
    left_chan = saved_fwd['chan_pair'][0]
    right_chan = saved_fwd['chan_pair'][1]
    if incoming:
        d_left = jnp.einsum('ckj,cij->cki', right_chan, d_chan, preferred_element_type=jnp.float32)
        d_right = jnp.einsum('cki,cij->ckj', left_chan, d_chan, preferred_element_type=jnp.float32)
    else:
        d_left = jnp.einsum('cij,cjk->cik', d_chan, right_chan, preferred_element_type=jnp.float32)
        d_right = jnp.einsum('cij,cik->cjk', d_chan, left_chan, preferred_element_type=jnp.float32)
    d_rows = to_rows(jnp.stack([d_left.astype(jnp.bfloat16), d_right.astype(jnp.bfloat16)]))
    d_left_f = d_rows[0].astype(jnp.float32) * mask_f
    d_right_f = d_rows[1].astype(jnp.float32) * mask_f
    sig_a = saved_fwd['sig_a']
    sig_b = saved_fwd['sig_b']
    d_proj = jnp.concatenate([d_left_f * sig_a, d_left_f * saved_fwd['lin_a'] * sig_a * (1.0 - sig_a), d_right_f * sig_b, d_right_f * saved_fwd['lin_b'] * sig_b * (1.0 - sig_b)], axis=0).astype(jnp.bfloat16)
    x_norm = saved_fwd['x_norm']
    g_w_proj = jnp.einsum('ijd,eij->de', x_norm, d_proj, preferred_element_type=jnp.float32)
    g_w_gate = jnp.einsum('ijd,ije->de', x_norm, d_gate, preferred_element_type=jnp.float32)
    d_x = (jnp.einsum('eij,de->ijd', d_proj, w_proj, preferred_element_type=jnp.float32) + jnp.einsum('ije,de->ijd', d_gate, w_gate, preferred_element_type=jnp.float32)).astype(jnp.bfloat16)
    d_zf, g_ln_p = saved_fwd['pair_back'](d_x.astype(jnp.float32))
    d_prev = (d_newf + d_zf).astype(jnp.bfloat16)
    return d_prev, (g_ln_p, g_w_proj, g_w_gate, g_ln_q, g_w_out)


def solution(mesh):
    row_spec = P(('data', 'dap'), None, None)
    mask_spec = P(('data', 'dap'), None)
    full_spec = P()
    grad_spec = P('data', None, None)

    def device_step(pair_act, pair_mask, d_pair_out, ln_pair, w_proj, w_gate, ln_chan, w_out):
        mask_f = pair_mask.astype(jnp.float32)
        z_mid, saved_out = update_forward(pair_act, mask_f, ln_pair[0], w_proj[0], w_gate[0], ln_chan[0], w_out[0], False)
        pair_out, saved_in = update_forward(z_mid, mask_f, ln_pair[1], w_proj[1], w_gate[1], ln_chan[1], w_out[1], True)
        d_mid, grads_in = update_backward(d_pair_out, saved_in, mask_f, w_proj[1], w_gate[1], w_out[1], True)
        d_pair, grads_out = update_backward(d_mid, saved_out, mask_f, w_proj[0], w_gate[0], w_out[0], False)
        local_grads = tuple(jnp.stack([grad_a, grad_b]) for grad_a, grad_b in zip(grads_out, grads_in))
        group_grads = lax.psum(local_grads, GROUP_AXIS)
        return (pair_out, d_pair) + tuple(grad_sum.astype(jnp.bfloat16) for grad_sum in group_grads)

    return jax.shard_map(device_step, mesh=mesh, in_specs=(row_spec, mask_spec, row_spec, full_spec, full_spec, full_spec, full_spec, full_spec), out_specs=(row_spec, row_spec, grad_spec, grad_spec, grad_spec, grad_spec, grad_spec), check_vma=False)
```

profile of v0, /device:TPU:0, one launch (start us, length us, event | category | flops | bytes accessed | tf_op | source)
XLA Modules:
  0.0 4608.0 jit_solution(15577269735730753521)
XLA Ops:
  44.7 57.3 %convolution_bitcast_fusion.1 = f32[512,96,768]{2,0,1:T(8,128)} fusion(bf16[2,128,512]{2,1,0:T(8,128)(2,1)S(1)} %copy-done.43, bf16[96,768,128]{1,2,0:T(8,128)(2,1)} %copy.239, f32[128]{0:T(128)S(1)} %get-tuple-element.118, f32[128]{0:T(128)S(1)} %get-tuple-element.119, f32[96,768]{1,0:T(8,128)S(1)} %fusion.114, f32[96,768]{1,0:T(8,128)S(1)} %broadcast_multiply_fusion.3), kind=kOutput, calls=%fused_computation.33 | convolution fusion | flops 9720299520 | bytes 170591232 | tf_op jit(solution)/shard_map/ijd,de->eij/dot_general | solution.py:39
  102.0 61.8 %fusion.86 = (bf16[1,128,96,768]{3,1,2,0:T(8,128)(2,1)}, bf16[1,128,96,768]{3,1,2,0:T(8,128)(2,1)}) fusion(f32[512,96,768]{2,0,1:T(8,128)} %convolution_bitcast_fusion.1, f32[96,768]{1,0:T(8,128)S(1)} %convert_element_type.227), kind=kLoop, calls=%fused_computation.149 | loop fusion | flops 113246208 | bytes 189038592 | tf_op jit(solution)/shard_map/stack | solution.py:46
  189.8 35.1 copy.244
  224.9 420.4 %all_to_all.114 = bf16[2,128,96,768]{3,2,0,1:T(8,128)(2,1)} all-to-all(bf16[2,128,96,768]{3,2,0,1:T(8,128)(2,1)} %copy.244), channel_id=1, replica_groups=mesh['data'=1,'dap'=8] {'dap'}, dimensions={1} | all-to-all | bytes 75497472 | tf_op jit(solution)/shard_map/all_to_all | solution.py:27
  753.9 205.0 %all-to-all-done.1 = bf16[16,768,768]{2,0,1:T(8,128)(2,1)} async-done(((bf16[16,768,768]{2,0,1:T(8,128)(2,1)}), bf16[16,768,768]{2,0,1:T(8,128)(2,1)}, u32[]{:S(2)}, u32[]{:S(2)}) %all-to-all-start.1) | async-done | bytes 18874400 | tf_op jit(solution)/shard_map/all_to_all | solution.py:32
  1022.7 48.8 %convert_reduce_fusion.2 = (f32[96,768]{1,0:T(8,128)S(1)}, bf16[96,768,128]{1,2,0:T(8,128)(2,1)}, f32[96,768,128]{1,2,0:T(8,128)}) fusion(f32[96,768,128]{1,2,0:T(8,128)} %fusion.94, bf16[96,768,128]{1,2,0:T(8,128)(2,1)} %copy.239, bf16[2,128,128]{2,1,0:T(8,128)(2,1)S(1)} %copy-done.47, f32[128]{0:T(128)S(1)} %copy-done.64, f32[128]{0:T(128)S(1)} %copy-done.56, ...), kind=kOutput, calls=%fused_computation.20 | convolution fusion | flops 2557403136 | bytes 133039104 | tf_op jit(solution)/shard_map/ijd,de->ije/dot_general | solution.py:40
  1102.5 56.2 %convolution_bitcast_fusion = f32[512,96,768]{2,0,1:T(8,128)} fusion(bf16[96,768,128]{1,2,0:T(8,128)(2,1)} %fusion.21, bf16[2,128,512]{2,1,0:T(8,128)(2,1)S(1)} %copy-done.44), kind=kOutput, calls=%fused_computation.32 | convolution fusion | flops 9663676416 | bytes 170000384 | tf_op jit(solution)/shard_map/ijd,de->eij/dot_general | solution.py:39
  1158.6 61.9 %fusion.88 = (bf16[1,128,96,768]{3,1,2,0:T(8,128)(2,1)}, bf16[1,128,96,768]{3,1,2,0:T(8,128)(2,1)}) fusion(f32[512,96,768]{2,0,1:T(8,128)} %convolution_bitcast_fusion, f32[96,768]{1,0:T(8,128)S(1)} %copy-done.21), kind=kLoop, calls=%fused_computation.151 | loop fusion | flops 113246208 | bytes 189038592 | tf_op jit(solution)/shard_map/stack | solution.py:46
  1246.5 35.3 copy.257
  1281.8 419.1 %all_to_all.115 = bf16[2,128,96,768]{3,2,0,1:T(8,128)(2,1)} all-to-all(bf16[2,128,96,768]{3,2,0,1:T(8,128)(2,1)} %copy.257), channel_id=1, replica_groups=mesh['data'=1,'dap'=8] {'dap'}, dimensions={1} | all-to-all | bytes 75497472 | tf_op jit(solution)/shard_map/all_to_all | solution.py:27
  1880.1 158.9 %all-to-all-done.3 = bf16[16,768,768]{2,0,1:T(8,128)(2,1)} async-done(((bf16[16,768,768]{2,0,1:T(8,128)(2,1)}), bf16[16,768,768]{2,0,1:T(8,128)(2,1)}, u32[]{:S(2)}, u32[]{:S(2)}) %all-to-all-start.3) | async-done | bytes 18874400 | tf_op jit(solution)/shard_map/all_to_all | solution.py:32
  2103.8 36.9 copy.272
  2140.7 40.7 fusion.25
  2181.5 48.5 %fusion.26 = (f32[128]{0:T(128)}, f32[96,768]{1,0:T(8,128)S(1)}) fusion(bf16[96,768,128]{2,1,0:T(8,128)(2,1)} %get-tuple-element.113, f32[128,96,768]{0,2,1:T(8,128)} %copy.272, f32[96,768]{1,0:T(8,128)S(1)} %broadcast_multiply_fusion, f32[96,768]{1,0:T(8,128)S(1)} %get-tuple-element.94, f32[96,768]{1,0:T(8,128)S(1)} %get-tuple-element.93, f32[128]{0:T(128)S(1)} %copy-done.53), kind=kLoop, calls=%fused_computation.56 | loop fusion | flops 103735168 | bytes 57803776 | tf_op jit(solution)/shard_map/transpose(jvp())/reduce_sum | solution.py:14
  2230.1 46.3 %add_convert_fusion.5 = bf16[128,96,768]{0,2,1:T(8,128)(2,1)} fusion(f32[96,768]{1,0:T(8,128)S(1)} %negate_multiply_fusion.3, f32[96,768]{1,0:T(8,128)S(1)} %get-tuple-element.93, f32[128,96,768]{0,2,1:T(8,128)} %copy.272, f32[96,768]{1,0:T(8,128)S(1)} %broadcast_multiply_fusion, f32[96,768]{1,0:T(8,128)S(1)} %get-tuple-element.94, f32[128]{0:T(128)S(1)} %copy-done.53, ...), kind=kLoop, calls=%fused_computation.134 | loop fusion | flops 84934656 | bytes 76677632 | tf_op jit(solution)/shard_map/convert_element_type | solution.py:68
  2300.9 209.6 %all_to_all.116 = bf16[128,96,768]{2,1,0:T(8,128)(2,1)S(1)} all-to-all(bf16[128,96,768]{2,1,0:T(8,128)(2,1)} %copy.273), channel_id=1, replica_groups=mesh['data'=1,'dap'=8] {'dap'}, dimensions={0} | all-to-all | bytes 37748736 | tf_op jit(solution)/shard_map/all_to_all | solution.py:27
  2599.9 35.0 copy.275
  2666.1 36.9 copy.286
  2722.1 43.8 fusion.37
  2765.9 284.3 %all-to-all-done.5 = bf16[2,16,768,768]{3,1,0,2:T(8,128)(2,1)} async-done(((bf16[2,16,768,768]{3,1,0,2:T(8,128)(2,1)}), bf16[2,16,768,768]{3,1,0,2:T(8,128)(2,1)}, u32[]{:S(2)}, u32[]{:S(2)}) %all-to-all-start.5) | async-done | bytes 37748768 | tf_op jit(solution)/shard_map/all_to_all | solution.py:32
  3101.2 84.7 %fusion.78 = (bf16[128,96,768]{2,0,1:T(8,128)(2,1)}, bf16[128,96,768]{2,0,1:T(8,128)(2,1)}, bf16[128,96,768]{2,0,1:T(8,128)(2,1)}, bf16[128,96,768]{2,0,1:T(8,128)(2,1)}) fusion(bf16[128,96,768]{2,0,1:T(8,128)(2,1)} %bitcast.307, f32[96,768]{1,0:T(8,128)S(1)} %copy-done.22, f32[512,96,768]{2,0,1:T(8,128)} %convolution_bitcast_fusion, ...), kind=kLoop, calls=%fused_computation.120 | loop fusion | flops 226492416 | bytes 264536064 | tf_op jit(solution)/shard_map/convert.18
  3186.0 39.3 fusion.109
  3288.3 56.3 %fusion.43 = (bf16[96,768,128]{1,2,0:T(8,128)(2,1)}, bf16[96,768,128]{1,2,0:T(8,128)(2,1)}) fusion(f32[96,768,128]{1,2,0:T(8,128)} %get-tuple-element.111, f32[96,768,128]{1,2,0:T(8,128)} %fusion.94, f32[96,768]{1,0:T(8,128)S(1)} %negate_multiply_fusion.2, f32[96,768]{1,0:T(8,128)S(1)} %multiply_multiply_fusion.2, f32[96,768]{1,0:T(8,128)S(1)} %copy-done.13, ...), kind=kLoop, calls=%fused_computation.73 | loop fusion | flops 169869312 | bytes 171049472 | tf_op jit(solution)/shard_map/convert_element_type | solution.py:63
  3344.7 40.9 fusion.24
  3385.7 48.5 %fusion.27 = (f32[128]{0:T(128)}, f32[96,768]{1,0:T(8,128)S(1)}) fusion(bf16[96,768,128]{2,1,0:T(8,128)(2,1)} %get-tuple-element.116, f32[128,96,768]{0,2,1:T(8,128)} %copy.286, f32[96,768]{1,0:T(8,128)S(1)} %copy-done.3, f32[96,768]{1,0:T(8,128)S(1)} %copy-done.15, f32[96,768]{1,0:T(8,128)S(1)} %multiply_multiply_fusion.1, f32[128]{0:T(128)S(1)} %copy-done.51), kind=kLoop, calls=%fused_computation.57 | loop fusion | flops 103735168 | bytes 57803776 | tf_op jit(solution)/shard_map/transpose(jvp())/reduce_sum | solution.py:14
  3434.3 46.3 %add_convert_fusion.3 = bf16[128,96,768]{0,2,1:T(8,128)(2,1)} fusion(f32[96,768]{1,0:T(8,128)S(1)} %negate_multiply_fusion.1, f32[96,768]{1,0:T(8,128)S(1)} %multiply_multiply_fusion.1, f32[128,96,768]{0,2,1:T(8,128)} %copy.286, f32[96,768]{1,0:T(8,128)S(1)} %copy-done.3, f32[96,768]{1,0:T(8,128)S(1)} %copy-done.15, f32[128]{0:T(128)S(1)} %copy-done.51, ...), kind=kLoop, calls=%fused_computation.132 | loop fusion | flops 84934656 | bytes 76677632 | tf_op jit(solution)/shard_map/convert_element_type | solution.py:68
  3505.0 209.3 %all_to_all.117 = bf16[128,96,768]{2,1,0:T(8,128)(2,1)S(1)} all-to-all(bf16[128,96,768]{2,1,0:T(8,128)(2,1)} %copy.287), channel_id=1, replica_groups=mesh['data'=1,'dap'=8] {'dap'}, dimensions={0} | all-to-all | bytes 37748736 | tf_op jit(solution)/shard_map/all_to_all | solution.py:27
  3988.6 38.8 fusion.110
  4027.4 223.5 %all-to-all-done.7 = bf16[2,16,768,768]{3,1,0,2:T(8,128)(2,1)} async-done(((bf16[2,16,768,768]{3,1,0,2:T(8,128)(2,1)}), bf16[2,16,768,768]{3,1,0,2:T(8,128)(2,1)}, u32[]{:S(2)}, u32[]{:S(2)}) %all-to-all-start.7) | async-done | bytes 37748768 | tf_op jit(solution)/shard_map/all_to_all | solution.py:32
  4301.8 84.9 %fusion.66 = (bf16[128,96,768]{2,0,1:T(8,128)(2,1)}, bf16[128,96,768]{2,0,1:T(8,128)(2,1)}, bf16[128,96,768]{2,0,1:T(8,128)(2,1)}, bf16[128,96,768]{2,0,1:T(8,128)(2,1)}) fusion(bf16[128,96,768]{2,0,1:T(8,128)(2,1)} %bitcast.305, f32[96,768]{1,0:T(8,128)S(1)} %copy-done.23, f32[512,96,768]{2,0,1:T(8,128)} %convolution_bitcast_fusion.1, ...), kind=kLoop, calls=%fused_computation.106 | loop fusion | flops 226492416 | bytes 264536064 | tf_op jit(solution)/shard_map/convert.14
  4386.7 36.7 fusion.111
  4423.5 39.1 fusion.107
  (291 shorter events, 1316.1 us)
Async XLA Ops:
  2.3 99.7 %copy-start.20 = (f32[96,768]{1,0:T(8,128)}, f32[96,768]{1,0:T(8,128)S(1)}, u32[]{:S(2)}) copy-start(f32[96,768]{1,0:T(8,128)S(1)} %convert_element_type.227) | copy-start | bytes 884740
  34.7 67.3 %copy-start.8 = (f32[96,768]{1,0:T(8,128)}, f32[96,768]{1,0:T(8,128)S(1)}, u32[]{:S(2)}) copy-start(f32[96,768]{1,0:T(8,128)S(1)} %broadcast_multiply_fusion.3) | copy-start | bytes 884740
  44.1 57.9 %copy-start.24 = (f32[96,768]{1,0:T(8,128)}, f32[96,768]{1,0:T(8,128)S(1)}, u32[]{:S(2)}) copy-start(f32[96,768]{1,0:T(8,128)S(1)} %fusion.114) | copy-start | bytes 884740
  44.6 57.3 %copy-start.55 = (f32[128]{0:T(128)}, f32[128]{0:T(128)S(1)}, u32[]{:S(2)}) copy-start(f32[128]{0:T(128)S(1)} %get-tuple-element.119) | copy-start | bytes 1540
  44.7 57.4 %copy-start.63 = (f32[128]{0:T(128)}, f32[128]{0:T(128)S(1)}, u32[]{:S(2)}) copy-start(f32[128]{0:T(128)S(1)} %get-tuple-element.118) | copy-start | bytes 1540
  747.5 211.4 %all-to-all-start.1 = ((bf16[16,768,768]{2,0,1:T(8,128)(2,1)}), bf16[16,768,768]{2,0,1:T(8,128)(2,1)}, u32[]{:S(2)}, u32[]{:S(2)}) async-start(bf16[16,768,768]{2,0,1:T(8,128)(2,1)} %copy.246), calls=%async_computation.1 | async-start | bytes 37748736 | tf_op jit(solution)/shard_map/all_to_all | solution.py:32
  1022.6 59.0 %copy-start.61 = (f32[128]{0:T(128)S(1)}, f32[128]{0:T(128)}, u32[]{:S(2)}) copy-start(f32[128]{0:T(128)} %get-tuple-element.105) | copy-start | bytes 1540
  1022.6 59.0 %copy-start.75 = (f32[128]{0:T(128)S(1)}, f32[128]{0:T(128)}, u32[]{:S(2)}) copy-start(f32[128]{0:T(128)} %get-tuple-element.106) | copy-start | bytes 1540
  1102.5 56.2 %copy-start.21 = (f32[96,768]{1,0:T(8,128)S(1)}, f32[96,768]{1,0:T(8,128)}, u32[]{:S(2)}) copy-start(f32[96,768]{1,0:T(8,128)} %copy-done.20) | copy-start | bytes 884740
  1827.6 211.4 %all-to-all-start.3 = ((bf16[16,768,768]{2,0,1:T(8,128)(2,1)}), bf16[16,768,768]{2,0,1:T(8,128)(2,1)}, u32[]{:S(2)}, u32[]{:S(2)}) async-start(bf16[16,768,768]{2,0,1:T(8,128)(2,1)} %copy.262), calls=%async_computation.3 | async-start | bytes 37748736 | tf_op jit(solution)/shard_map/all_to_all | solution.py:32
  2070.0 160.0 %copy-start.5 = (f32[96,768]{1,0:T(8,128)}, f32[96,768]{1,0:T(8,128)S(1)}, u32[]{:S(2)}) copy-start(f32[96,768]{1,0:T(8,128)S(1)} %broadcast_multiply_fusion) | copy-start | bytes 884740
  2181.4 48.7 %slice-start = ((s8[18874368]{0:T(1024)(128)(4,1)}), s8[4194304]{0:T(1024)(128)(4,1)S(1)}, s32[]{:S(2)}) async-start(s8[18874368]{0:T(1024)(128)(4,1)} %bitcast.292), calls=%async_computation.8 | async-start | bytes 8388608
  2181.5 48.6 %copy-start.17 = (f32[96,768]{1,0:T(8,128)}, f32[96,768]{1,0:T(8,128)S(1)}, u32[]{:S(2)}) copy-start(f32[96,768]{1,0:T(8,128)S(1)} %get-tuple-element.94) | copy-start | bytes 884740
  2181.5 48.6 %slice-start.1 = ((s8[18874368]{0:T(1024)(128)(4,1)}), s8[4194304]{0:T(1024)(128)(4,1)S(1)}, s32[]{:S(2)}) async-start(s8[18874368]{0:T(1024)(128)(4,1)} %bitcast.292), calls=%async_computation.9 | async-start | bytes 8388608
  2181.5 48.6 %slice-start.2 = ((s8[18874368]{0:T(1024)(128)(4,1)}), s8[4194304]{0:T(1024)(128)(4,1)S(1)}, s32[]{:S(2)}) async-start(s8[18874368]{0:T(1024)(128)(4,1)} %bitcast.292), calls=%async_computation.10 | async-start | bytes 8388608
  2181.5 48.6 %slice-start.3 = ((s8[18874368]{0:T(1024)(128)(4,1)}), s8[4194304]{0:T(1024)(128)(4,1)S(1)}, s32[]{:S(2)}) async-start(s8[18874368]{0:T(1024)(128)(4,1)} %bitcast.292), calls=%async_computation.11 | async-start | bytes 8388608
  2181.5 48.6 %slice-start.4 = ((s8[18874368]{0:T(1024)(128)(4,1)}), s8[2097152]{0:T(1024)(128)(4,1)S(1)}, s32[]{:S(2)}) async-start(s8[18874368]{0:T(1024)(128)(4,1)} %bitcast.292), calls=%async_computation.12 | async-start | bytes 4194304
  2634.9 415.3 %all-to-all-start.5 = ((bf16[2,16,768,768]{3,1,0,2:T(8,128)(2,1)}), bf16[2,16,768,768]{3,1,0,2:T(8,128)(2,1)}, u32[]{:S(2)}, u32[]{:S(2)}) async-start(bf16[2,16,768,768]{3,1,0,2:T(8,128)(2,1)} %copy.275), calls=%async_computation.5 | async-start | bytes 75497472 | tf_op jit(solution)/shard_map/all_to_all | solution.py:32
  3101.2 84.8 %copy-start.45 = (bf16[2,128,512]{2,1,0:T(8,128)(2,1)S(1)}, bf16[2,128,512]{2,1,0:T(8,128)(2,1)}, u32[]{:S(2)}) copy-start(bf16[2,128,512]{2,1,0:T(8,128)(2,1)} %param.12) | copy-start | bytes 786436
  3288.3 56.3 %copy-start.3 = (f32[96,768]{1,0:T(8,128)S(1)}, f32[96,768]{1,0:T(8,128)}, u32[]{:S(2)}) copy-start(f32[96,768]{1,0:T(8,128)} %copy-done.2) | copy-start | bytes 884740
  3288.3 56.3 %copy-start.41 = (bf16[2,128,128]{2,1,0:T(8,128)(2,1)S(1)}, bf16[2,128,128]{2,1,0:T(8,128)(2,1)}, u32[]{:S(2)}) copy-start(bf16[2,128,128]{2,1,0:T(8,128)(2,1)} %param.15) | copy-start | bytes 196612
  3288.3 56.3 %copy-start.51 = (f32[128]{0:T(128)S(1)}, f32[128]{0:T(128)}, u32[]{:S(2)}) copy-start(f32[128]{0:T(128)} %get-tuple-element.122) | copy-start | bytes 1540
  3385.5 48.7 %slice-start.5 = ((s8[18874368]{0:T(1024)(128)(4,1)}), s8[4194304]{0:T(1024)(128)(4,1)S(1)}, s32[]{:S(2)}) async-start(s8[18874368]{0:T(1024)(128)(4,1)} %bitcast.294), calls=%async_computation.13 | async-start | bytes 8388608
  3385.7 48.6 %slice-start.6 = ((s8[18874368]{0:T(1024)(128)(4,1)}), s8[4194304]{0:T(1024)(128)(4,1)S(1)}, s32[]{:S(2)}) async-start(s8[18874368]{0:T(1024)(128)(4,1)} %bitcast.294), calls=%async_computation.14 | async-start | bytes 8388608
  3385.7 48.5 %slice-start.7 = ((s8[18874368]{0:T(1024)(128)(4,1)}), s8[4194304]{0:T(1024)(128)(4,1)S(1)}, s32[]{:S(2)}) async-start(s8[18874368]{0:T(1024)(128)(4,1)} %bitcast.294), calls=%async_computation.15 | async-start | bytes 8388608
  3385.7 48.5 %slice-start.8 = ((s8[18874368]{0:T(1024)(128)(4,1)}), s8[4194304]{0:T(1024)(128)(4,1)S(1)}, s32[]{:S(2)}) async-start(s8[18874368]{0:T(1024)(128)(4,1)} %bitcast.294), calls=%async_computation.16 | async-start | bytes 8388608
  3385.7 48.5 %slice-start.9 = ((s8[18874368]{0:T(1024)(128)(4,1)}), s8[2097152]{0:T(1024)(128)(4,1)S(1)}, s32[]{:S(2)}) async-start(s8[18874368]{0:T(1024)(128)(4,1)} %bitcast.294), calls=%async_computation.17 | async-start | bytes 4194304
  3835.6 415.3 %all-to-all-start.7 = ((bf16[2,16,768,768]{3,1,0,2:T(8,128)(2,1)}), bf16[2,16,768,768]{3,1,0,2:T(8,128)(2,1)}, u32[]{:S(2)}, u32[]{:S(2)}) async-start(bf16[2,16,768,768]{3,1,0,2:T(8,128)(2,1)} %copy.290), calls=%async_computation.7 | async-start | bytes 75497472 | tf_op jit(solution)/shard_map/all_to_all | solution.py:32
  4301.7 84.9 %copy-start.11 = (f32[96,768]{1,0:T(8,128)S(1)}, f32[96,768]{1,0:T(8,128)}, u32[]{:S(2)}) copy-start(f32[96,768]{1,0:T(8,128)} %copy-done.8) | copy-start | bytes 884740
  4301.8 84.9 %copy-start.27 = (f32[96,768]{1,0:T(8,128)S(1)}, f32[96,768]{1,0:T(8,128)}, u32[]{:S(2)}) copy-start(f32[96,768]{1,0:T(8,128)} %copy-done.24) | copy-start | bytes 884740
  4301.8 84.9 %copy-start.58 = (f32[128]{0:T(128)S(1)}, f32[128]{0:T(128)}, u32[]{:S(2)}) copy-start(f32[128]{0:T(128)} %copy-done.55) | copy-start | bytes 1540
  4301.8 84.9 %copy-start.66 = (f32[128]{0:T(128)S(1)}, f32[128]{0:T(128)}, u32[]{:S(2)}) copy-start(f32[128]{0:T(128)} %copy-done.63) | copy-start | bytes 1540
  (64 other events, 1695.8 us)
where the time goes:
time: 4620 us; the launch traced here: 4610 us
  blocking collectives  1290 us (28%)
  waiting for transfers between devices  872 us (19%)
  other arithmetic  865 us (19%)
  matrix products  823 us (18%)
  local copies, waits for them, and re-layouts  734 us (16%)
    all_to_all x4, blocking collectives, to_channels(): lax.all_to_all(row_blocks, GROUP_AXIS, chan_dim, chan_dim + 1, tiled=True)  1260 us
    all_to_all x4, waiting for transfers between devices, to_rows(): lax.all_to_all(chan_blocks, GROUP_AXIS, chan_dim + 1, chan_dim, tiled=True)  872 us
    reduce_sum x6, other arithmetic, layer_norm(): return centered * lax.rsqrt(variance + LN_EPS) * gain_vec + shift_vec  177 us
    another operation x4, other arithmetic, update_forward(): chan_pair = to_channels(jnp.stack([left_proj, right_proj]))  176 us
    another operation x2, other arithmetic  170 us
    convert_element_type x4, local copies, waits for them, and re-layouts, update_forward(): t_rows.astype(jnp.float32)  116 us
    dot_general x2, matrix products, update_forward(): jnp.einsum('ijd,de->eij', x_norm, w_proj, preferred_element_type=jnp.floa...  113 us
    unnamed x188, local copies, waits for them, and re-layouts  102 us
  transfers between devices with their start and end apart: 4, of which 4 were waited for; matrix products, arithmetic and copies ran while one was open for 8% of the time, Pallas kernels for 0%

commit v1 on v0

v1 whole, which is shorter than its diff:
```python
import functools

import jax
import jax.numpy as jnp
from jax import lax
from jax.experimental import pallas as pl
from jax.experimental.pallas import tpu as pltpu
from jax.sharding import PartitionSpec as P

LN_EPS = 1e-5
AXIS = 'dap'
NDEV = 8
N = 768
C = 128
G = C // NDEV
ROWS = N // NDEV
R = 3
RC = ROWS // R
M = NDEV * RC
LB = 256
RB = 4
BF = jnp.bfloat16
F32 = jnp.float32


def dotg(lhs, rhs, lc, rc):
    return lax.dot_general(lhs, rhs, (((lc,), (rc,)), ((), ())), preferred_element_type=F32)


def norm_z(z_val, ln_p):
    zf = z_val.astype(F32)
    centered = zf - jnp.mean(zf, axis=1, keepdims=True)
    rstd = lax.rsqrt(jnp.mean(centered * centered, axis=1, keepdims=True) + LN_EPS)
    hat = centered * rstd
    return (hat * ln_p[0:1] + ln_p[1:2]).astype(BF), hat, rstd


def norm_t(t_val, gain, shift):
    tf = t_val.astype(F32)
    centered = tf - jnp.mean(tf, axis=0, keepdims=True)
    rstd = lax.rsqrt(jnp.mean(centered * centered, axis=0, keepdims=True) + LN_EPS)
    hat = centered * rstd
    return (hat * gain + shift).astype(BF), hat, rstd


def project(x_val, wp_t):
    proj = dotg(wp_t, x_val, 1, 1)
    return proj[0:C], jax.nn.sigmoid(proj[C:2 * C]), proj[2 * C:3 * C], jax.nn.sigmoid(proj[3 * C:4 * C])


def store_ab(ab_ref, row, cols, x_val, wp_t, mask):
    lin_a, sig_a, lin_b, sig_b = project(x_val, wp_t)
    ab_ref[:, 0, row, :, cols] = (mask * sig_a * lin_a).astype(BF).reshape(NDEV, G, LB)
    ab_ref[:, 1, row, :, cols] = (mask * sig_b * lin_b).astype(BF).reshape(NDEV, G, LB)


def gate_update(x_val, y_val, w_gate, w_out):
    return jax.nn.sigmoid(dotg(x_val, w_gate, 1, 0)), dotg(y_val, w_out, 0, 0)


def lane_fold(val):
    return val[:, 0:128] + val[:, 128:256]


def row_fold(val):
    return jnp.sum(val.reshape(LB // 8, 8, C), axis=0)


def finish_back(d_f, gate, upd, x_val, y_val, t_hat, t_rstd, gain, w_out, dt_ref, dg_ref, row, cols, acc):
    gwo_ref, gwg_ref, glq_ref = acc
    d_gate = (d_f * upd * gate * (1.0 - gate)).astype(BF)
    d_upd = (d_f * gate).astype(BF)
    dg_ref[row, cols, :] = d_gate
    gwo_ref[...] += dotg(y_val, d_upd, 1, 0)
    gwg_ref[...] += dotg(x_val, d_gate, 0, 0)
    d_y = dotg(w_out, d_upd, 1, 1).astype(BF).astype(F32)
    glq_ref[0] += lane_fold(d_y * t_hat)
    glq_ref[1] += lane_fold(d_y)
    d_hat = d_y * gain
    m_one = jnp.mean(d_hat, axis=0, keepdims=True)
    m_two = jnp.mean(d_hat * t_hat, axis=0, keepdims=True)
    d_t = t_rstd * (d_hat - m_one - t_hat * m_two)
    dt_ref[:, row, :, cols] = d_t.astype(BF).reshape(NDEV, G, LB)


def project_back(x_val, hat, rstd, ln_p, wp_t, w_gate, mask, d_a, d_b, d_gate, d_f, acc):
    gwp_ref, glp_ref = acc
    lin_a, sig_a, lin_b, sig_b = project(x_val, wp_t)
    d_a = d_a.astype(F32) * mask
    d_b = d_b.astype(F32) * mask
    da_s = d_a * sig_a
    db_s = d_b * sig_b
    d_proj = jnp.concatenate([da_s.astype(BF), (da_s * lin_a * (1.0 - sig_a)).astype(BF), db_s.astype(BF), (db_s * lin_b * (1.0 - sig_b)).astype(BF)], axis=0)
    gwp_ref[...] += dotg(d_proj, x_val, 1, 0)
    d_x = (dotg(d_proj, wp_t, 0, 0) + dotg(d_gate, w_gate, 1, 1)).astype(BF).astype(F32)
    glp_ref[0] += row_fold(d_x * hat)
    glp_ref[1] += row_fold(d_x)
    d_hat = d_x * ln_p[0:1]
    m_one = jnp.mean(d_hat, axis=1, keepdims=True)
    m_two = jnp.mean(d_hat * hat, axis=1, keepdims=True)
    return (d_f + rstd * (d_hat - m_one - hat * m_two)).astype(BF)


def each_block(body):
    @pl.loop(0, RB)
    def _(row):
        for q in range(N // LB):
            body(row, slice(q * LB, (q + 1) * LB))


def zero_first(refs):
    @pl.when(pl.program_id(0) == 0)
    def _():
        for ref in refs:
            ref[...] = jnp.zeros_like(ref)


def load_mask(m_ref, row, cols):
    return m_ref[row, :, cols].astype(F32)


def load_t(t_ref, row, cols):
    return t_ref[:, row, :, cols].reshape(C, LB)


def body_a(z_ref, m_ref, lnp_ref, wp_ref, ab_ref):
    def one(row, cols):
        x_val, _, _ = norm_z(z_ref[row, cols, :], lnp_ref[...])
        store_ab(ab_ref, row, cols, x_val, wp_ref[...], load_mask(m_ref, row, cols))
    each_block(one)


def body_b(z_ref, t_ref, m_ref, lnp_ref, wg_ref, lnq_ref, wo_ref, lnp2_ref, wp2_ref, zn_ref, ab_ref):
    def one(row, cols):
        z_val = z_ref[row, cols, :]
        x_val, _, _ = norm_z(z_val, lnp_ref[...])
        y_val, _, _ = norm_t(load_t(t_ref, row, cols), lnq_ref[0], lnq_ref[1])
        gate, upd = gate_update(x_val, y_val, wg_ref[...], wo_ref[...])
        z_new = (z_val.astype(F32) + gate * upd).astype(BF)
        zn_ref[row, cols, :] = z_new
        x_new, _, _ = norm_z(z_new, lnp2_ref[...])
        store_ab(ab_ref, row, cols, x_new, wp2_ref[...], load_mask(m_ref, row, cols))
    each_block(one)


def body_c(z_ref, t_ref, g_ref, lnp_ref, wg_ref, lnq_ref, wo_ref, *rest):
    zn_ref, dt_ref, dg_ref, gwo_ref, gwg_ref, glq_ref = rest[-6:]
    zero_first((gwo_ref, gwg_ref, glq_ref))

    def one(row, cols):
        z_val = z_ref[row, cols, :]
        x_val, _, _ = norm_z(z_val, lnp_ref[...])
        y_val, t_hat, t_rstd = norm_t(load_t(t_ref, row, cols), lnq_ref[0], lnq_ref[1])
        gate, upd = gate_update(x_val, y_val, wg_ref[...], wo_ref[...])
        zn_ref[row, cols, :] = (z_val.astype(F32) + gate * upd).astype(BF)
        d_f = g_ref[row, cols, :].astype(F32)
        finish_back(d_f, gate, upd, x_val, y_val, t_hat, t_rstd, lnq_ref[0], wo_ref[...], dt_ref, dg_ref, row, cols, (gwo_ref, gwg_ref, glq_ref))
    each_block(one)


def body_d(zm_ref, dab_ref, dgm_ref, g_ref, m_ref, lnp2_ref, wp2_ref, wg2_ref, z_ref, t_ref, lnp_ref, wg_ref, lnq_ref, wo_ref,
           dm_ref, dt_ref, dg_ref, gwp_ref, glp_ref, gwo_ref, gwg_ref, glq_ref):
    zero_first((gwp_ref, glp_ref, gwo_ref, gwg_ref, glq_ref))

    def one(row, cols):
        x2, hat2, rstd2 = norm_z(zm_ref[row, cols, :], lnp2_ref[...])
        d_mid = project_back(x2, hat2, rstd2, lnp2_ref[...], wp2_ref[...], wg2_ref[...], load_mask(m_ref, row, cols),
                             dab_ref[:, 0, row, :, cols].reshape(C, LB), dab_ref[:, 1, row, :, cols].reshape(C, LB),
                             dgm_ref[row, cols, :], g_ref[row, cols, :].astype(F32), (gwp_ref, glp_ref))
        dm_ref[row, cols, :] = d_mid
        x_val, _, _ = norm_z(z_ref[row, cols, :], lnp_ref[...])
        y_val, t_hat, t_rstd = norm_t(load_t(t_ref, row, cols), lnq_ref[0], lnq_ref[1])
        gate, upd = gate_update(x_val, y_val, wg_ref[...], wo_ref[...])
        finish_back(d_mid.astype(F32), gate, upd, x_val, y_val, t_hat, t_rstd, lnq_ref[0], wo_ref[...], dt_ref, dg_ref, row, cols, (gwo_ref, gwg_ref, glq_ref))
    each_block(one)


def body_e(z_ref, da_ref, db_ref, dg_ref, dm_ref, m_ref, lnp_ref, wp_ref, wg_ref, *rest):
    dz_ref, gwp_ref, glp_ref = rest[-3:]
    zero_first((gwp_ref, glp_ref))

    def one(row, cols):
        x_val, hat, rstd = norm_z(z_ref[row, cols, :], lnp_ref[...])
        dz_ref[row, cols, :] = project_back(x_val, hat, rstd, lnp_ref[...], wp_ref[...], wg_ref[...], load_mask(m_ref, row, cols),
                                            load_t(da_ref, row, cols), load_t(db_ref, row, cols),
                                            dg_ref[row, cols, :], dm_ref[row, cols, :].astype(F32), (gwp_ref, glp_ref))
    each_block(one)


STEPS = RC // RB


def full_rows(chunk):
    return pl.BlockSpec((RB, N, C), lambda i: (chunk * STEPS + i, 0, 0))


def mask_rows(chunk):
    return pl.BlockSpec((RB, 1, N), lambda i: (chunk * STEPS + i, 0, 0))


PIECE = pl.BlockSpec((RB, N, C), lambda i: (i, 0, 0))
CHAN = pl.BlockSpec((NDEV, RB, G, N), lambda i: (0, i, 0, 0))
CHAN2 = pl.BlockSpec((NDEV, 2, RB, G, N), lambda i: (0, 0, i, 0, 0))
CHAN_T = jax.ShapeDtypeStruct((NDEV, RC, G, N), BF)
CHAN2_T = jax.ShapeDtypeStruct((NDEV, 2, RC, G, N), BF)
PIECE_T = jax.ShapeDtypeStruct((RC, N, C), BF)
FULL_T = jax.ShapeDtypeStruct((ROWS, N, C), BF)


def whole(shape):
    return pl.BlockSpec(shape, lambda i: (0,) * len(shape))


def acc(shape):
    return whole(shape), jax.ShapeDtypeStruct(shape, F32)


GWP = acc((4 * C, C))
GLP = acc((2, 8, C))
GWO = acc((C, C))
GWG = acc((C, C))
GLQ = acc((2, C, 128))
ANY = pl.BlockSpec(memory_space=pl.ANY)


def call(body, name, grid, in_specs, outs, flops, args, aliases=None, scratch=()):
    return pl.pallas_call(
        body,
        grid=(grid,),
        in_specs=in_specs,
        out_specs=[spec for spec, _ in outs],
        out_shape=[shape for _, shape in outs],
        scratch_shapes=list(scratch),
        input_output_aliases=aliases or {},
        compiler_params=pltpu.CompilerParams(dimension_semantics=('arbitrary',), vmem_limit_bytes=58 * 1024 * 1024),
        cost_estimate=pl.CostEstimate(flops=flops, bytes_accessed=60_000_000, transcendentals=0),
        name=name,
    )(*args)


POS = RC * N
UNIT = 2 * POS * C * C


def place(dst, parts):
    for chunk, part in enumerate(parts):
        for dev in range(NDEV):
            dst[dev * ROWS + chunk * RC:dev * ROWS + (chunk + 1) * RC, :] = part[dev * RC:(dev + 1) * RC, :]


def split_rows(full, outs):
    for chunk, out in enumerate(outs):
        for dev in range(NDEV):
            out[dev * RC:(dev + 1) * RC, :] = full[dev * ROWS + chunk * RC:dev * ROWS + (chunk + 1) * RC, :]


def tri_rows(lhs, b0, b1, b2, out, full, *, rhs_dim):
    place(full, (b0, b1, b2))
    out[...] = dotg(lhs[...], full[...], 1, rhs_dim).astype(BF)


def tri_sum(a0, a1, a2, b0, b1, b2, o0, o1, o2):
    total = dotg(a0[...], b0[...], 0, 0) + dotg(a1[...], b1[...], 0, 0) + dotg(a2[...], b2[...], 0, 0)
    split_rows(total.astype(BF), (o0, o1, o2))


def tri_pair(a_r, b_r, d0, d1, d2, out, full):
    place(full, (d0, d1, d2))
    out[0] = dotg(b_r[...], full[...], 1, 1).astype(BF)
    out[1] = dotg(a_r[...], full[...], 1, 0).astype(BF)


SQ = None


def chan(which=None):
    if which is None:
        return pl.BlockSpec((None, M, N), lambda c: (c, 0, 0))
    return pl.BlockSpec((None, None, M, N), lambda c: (which, c, 0, 0))


TRI_T = jax.ShapeDtypeStruct((G, M, N), BF)
TRI = (pl.BlockSpec((None, M, N), lambda c: (c, 0, 0)), TRI_T)
TRI2 = (pl.BlockSpec((2, None, M, N), lambda c: (0, c, 0, 0)), jax.ShapeDtypeStruct((2, G, M, N), BF))
FULL = (pltpu.VMEM((N, N), BF),)
TRI_FLOPS = 2 * G * M * N * N


def arrive2(x):
    return jnp.transpose(x, (1, 3, 0, 2, 4)).reshape(2, G, M, N)


def arrive(x):
    return jnp.transpose(x, (2, 0, 1, 3)).reshape(G, M, N)


def leave(x):
    return jnp.transpose(x.reshape(G, NDEV, RC, N), (1, 2, 0, 3))


def leave2(x):
    return jnp.transpose(x.reshape(2, G, NDEV, RC, N), (2, 0, 3, 1, 4))


def exchange(x, name):
    with jax.named_scope(name):
        return lax.all_to_all(x, AXIS, 0, 0)


def device_step(pair_act, pair_mask, d_pair_out, ln_pair, w_proj, w_gate, ln_chan, w_out):
    mask = pair_mask.reshape(ROWS, 1, N)
    lnp = [ln_pair[u].astype(F32) for u in range(2)]
    wpt = [w_proj[u].T for u in range(2)]
    lnq = [jnp.broadcast_to(ln_chan[u].astype(F32)[:, :, None], (2, C, LB)) for u in range(2)]
    S_LNP, S_WP, S_W, S_LNQ = whole((2, C)), whole((4 * C, C)), whole((C, C)), whole((2, C, LB))
    rng = range(R)

    ab = [call(body_a, f'pos_a{r}', STEPS, [full_rows(r), mask_rows(r), S_LNP, S_WP], [(CHAN2, CHAN2_T)], 4 * UNIT,
               (pair_act, mask, lnp[0], wpt[0]))[0] for r in rng]
    ab = [arrive2(exchange(ab[r], f'x_ab{r}')) for r in rng]
    t_out = []
    for r in rng:
        t_r = call(functools.partial(tri_rows, rhs_dim=1), f'tri_of{r}', G, [chan(0)] + [chan(1)] * 3, [TRI], TRI_FLOPS,
                   (ab[r], ab[0], ab[1], ab[2]), scratch=FULL)[0]
        t_out.append(exchange(leave(t_r), f'x_t{r}'))

    z_mid, ab2 = [], []
    for r in rng:
        z_r, ab_r = call(body_b, f'pos_b{r}', STEPS,
                         [full_rows(r), CHAN, mask_rows(r), S_LNP, S_W, S_LNQ, S_W, S_LNP, S_WP],
                         [(PIECE, PIECE_T), (CHAN2, CHAN2_T)], 6 * UNIT,
                         (pair_act, t_out[r], mask, lnp[0], w_gate[0], lnq[0], w_out[0], lnp[1], wpt[1]))
        z_mid.append(z_r)
        ab2.append(arrive2(exchange(ab_r, f'x_ab2{r}')))
    t_in = call(tri_sum, 'tri_if', G, [chan(0)] * 3 + [chan(1)] * 3, [TRI] * 3, 3 * TRI_FLOPS, tuple(ab2) * 2)
    t_in = [exchange(leave(t_in[r]), f'x_t2{r}') for r in rng]

    pair_out = None
    d_t2, d_gate2, acc_c = [], [], []
    for r in rng:
        ins = [PIECE, CHAN, full_rows(r), S_LNP, S_W, S_LNQ, S_W]
        args = (z_mid[r], t_in[r], d_pair_out, lnp[1], w_gate[1], lnq[1], w_out[1])
        aliases = {}
        if pair_out is not None:
            aliases = {len(ins): 0}
            ins, args = ins + [ANY], args + (pair_out,)
        pair_out, dt_r, dg_r, *grads = call(body_c, f'pos_c{r}', STEPS, ins,
                                            [(full_rows(r), FULL_T), (CHAN, CHAN_T), (PIECE, PIECE_T), GWO, GWG, GLQ], 6 * UNIT,
                                            args, aliases)
        d_t2.append(arrive(exchange(dt_r, f'x_dt2{r}')))
        d_gate2.append(dg_r)
        acc_c.append(grads)

    d_mid, d_t, d_gate, acc_d = [], [], [], []
    for r in rng:
        dab = call(tri_pair, f'tri_ib{r}', G, [chan(0), chan(1)] + [chan()] * 3, [TRI2], 2 * TRI_FLOPS,
                   (ab2[r], ab2[r], d_t2[0], d_t2[1], d_t2[2]), scratch=FULL)[0]
        dab = exchange(leave2(dab), f'x_dab2{r}')
        dm_r, dt_r, dg_r, *grads = call(
            body_d, f'pos_d{r}', STEPS,
            [PIECE, CHAN2, PIECE, full_rows(r), mask_rows(r), S_LNP, S_WP, S_W, full_rows(r), CHAN, S_LNP, S_W, S_LNQ, S_W],
            [(PIECE, PIECE_T), (CHAN, CHAN_T), (PIECE, PIECE_T), GWP, GLP, GWO, GWG, GLQ], 18 * UNIT,
            (z_mid[r], dab, d_gate2[r], d_pair_out, mask, lnp[1], wpt[1], w_gate[1],
             pair_act, t_out[r], lnp[0], w_gate[0], lnq[0], w_out[0]))
        d_mid.append(dm_r)
        d_t.append(arrive(exchange(dt_r, f'x_dt{r}')))
        d_gate.append(dg_r)
        acc_d.append(grads)

    d_b = call(tri_sum, 'tri_ob', G, [chan()] * 3 + [chan(0)] * 3, [TRI] * 3, 3 * TRI_FLOPS, tuple(d_t) + tuple(ab))
    d_pair = None
    acc_e = []
    for r in rng:
        da_r = call(functools.partial(tri_rows, rhs_dim=0), f'tri_oa{r}', G, [chan()] + [chan(1)] * 3, [TRI], TRI_FLOPS,
                    (d_t[r], ab[0], ab[1], ab[2]), scratch=FULL)[0]
        da_r = exchange(leave(da_r), f'x_da{r}')
        db_r = exchange(leave(d_b[r]), f'x_db{r}')
        ins = [full_rows(r), CHAN, CHAN, PIECE, PIECE, mask_rows(r), S_LNP, S_WP, S_W]
        args = (pair_act, da_r, db_r, d_gate[r], d_mid[r], mask, lnp[0], wpt[0], w_gate[0])
        aliases = {}
        if d_pair is not None:
            aliases = {len(ins): 0}
            ins, args = ins + [ANY], args + (d_pair,)
        d_pair, *grads = call(body_e, f'pos_e{r}', STEPS, ins, [(full_rows(r), FULL_T), GWP, GLP], 13 * UNIT, args, aliases)
        acc_e.append(grads)

    total = lambda parts: [sum(vals[1:], vals[0]) for vals in zip(*parts)]
    gwo1, gwg1, glq1 = total(acc_c)
    gwp1, glp1, gwo0, gwg0, glq0 = total(acc_d)
    gwp0, glp0 = total(acc_e)
    local = (jnp.stack([glp0.sum(1), glp1.sum(1)]), jnp.stack([gwp0.T, gwp1.T]), jnp.stack([gwg0, gwg1]),
             jnp.stack([glq0.sum(2), glq1.sum(2)]), jnp.stack([gwo0, gwo1]))
    grads = lax.psum(local, AXIS)
    return (pair_out, d_pair) + tuple(val.astype(BF) for val in grads)


def solution(mesh):
    row_spec = P(('data', 'dap'), None, None)
    mask_spec = P(('data', 'dap'), None)
    full_spec = P()
    grad_spec = P('data', None, None)
    return jax.shard_map(device_step, mesh=mesh, in_specs=(row_spec, mask_spec, row_spec, full_spec, full_spec, full_spec, full_spec, full_spec), out_specs=(row_spec, row_spec, grad_spec, grad_spec, grad_spec, grad_spec, grad_spec), check_vma=False)
```

time: 4620 us -> 2980 us (0.65)
  blocking collectives: 1290 us -> 32.5 us
  Pallas kernels: 0 us -> 992 us
  other arithmetic: 865 us -> 3.37 us
  matrix products: 823 us -> 0 us
  waiting for transfers between devices: 872 us -> 1550 us
  local copies, waits for them, and re-layouts: 734 us -> 279 us
  starting transfers between devices: 22.8 us -> 102 us
    all_to_all x4 -> x0, blocking collectives: 1260 us -> none  [to_channels(): lax.all_to_all(row_blocks, GROUP_AXIS, chan_dim, chan_dim + 1, tiled=True)]
    pallas_call x0 -> x26, Pallas kernels: none -> 992 us  [call(): pl.pallas_call(body, grid=(grid,), in_specs=in_specs, out_specs=[spec for...]
    dot_general x24 -> x0, matrix products: 823 us -> none  [the longest x2 113 us: update_forward(): jnp.einsum('ijd,de->eij', x_norm, w_proj, preferred_element_type=jnp.floa...]
    all_to_all x4 -> x27, waiting for transfers between devices: 872 us -> 1550 us  [exchange(): return lax.all_to_all(x, AXIS, 0, 0)]
    another operation x17 -> x11, other arithmetic: 400 us -> 1.16 us  [the longest x3 1.07 us: device_step(): jnp.stack([gwp0.T, gwp1.T])]
    convert_element_type x12 -> x2, other arithmetic: 244 us -> 1.24 us  [the longest x1 1.24 us: device_step(): lnp = [ln_pair[u].astype(F32) for u in range(2)]]
    reduce_sum x13 -> x4, other arithmetic: 220 us -> 0.97 us  [the longest x1 0.72 us: device_step(): glp0.sum(1)]
    convert_element_type x10 -> x0, local copies, waits for them, and re-layouts: 218 us -> none  [the longest x4 116 us: update_forward(): t_rows.astype(jnp.float32)]
  transfers between devices with their start and end apart: 4 -> 27, of which waited for: 4 -> 24; matrix products, arithmetic and copies ran while one was open for 8% -> 7% of each run, Pallas kernels for 0% -> 29%
where the time goes in v1:
time: 2980 us; the launch traced here: 2960 us
  waiting for transfers between devices  1550 us (52%)
  Pallas kernels  992 us (33%)
  local copies, waits for them, and re-layouts  279 us (9%)
  starting transfers between devices  102 us (3%)
  blocking collectives  32.5 us (1%)
    all_to_all x27, waiting for transfers between devices, exchange(): return lax.all_to_all(x, AXIS, 0, 0)  1550 us
    pallas_call x26, Pallas kernels, call(): pl.pallas_call(body, grid=(grid,), in_specs=in_specs, out_specs=[spec for...  992 us
    pallas_call x12, local copies, waits for them, and re-layouts, call(): pl.pallas_call(body, grid=(grid,), in_specs=in_specs, out_specs=[spec for...  108 us
    all_to_all x27, starting transfers between devices, exchange(): return lax.all_to_all(x, AXIS, 0, 0)  102 us
    transpose x6, local copies, waits for them, and re-layouts, arrive2(): return jnp.transpose(x, (1, 3, 0, 2, 4)).reshape(2, G, M, N)  75.9 us
  transfers between devices with their start and end apart: 27, of which 24 were waited for; matrix products, arithmetic and copies ran while one was open for 7% of the time, Pallas kernels for 29%

profile of v1, /device:TPU:0, one launch (start us, length us, event | category | flops | bytes accessed | tf_op | source)
XLA Modules:
  0.0 2962.6 jit_solution(5529426139916806949)
XLA Ops:
  56.6 116.6 %all-to-all-done.2 = bf16[8,2,32,16,768]{4,3,2,1,0:T(8,128)(2,1)} async-done(((bf16[8,2,32,16,768]{4,3,2,1,0:T(8,128)(2,1)}), bf16[8,2,32,16,768]{4,3,2,1,0:T(8,128)(2,1)}, u32[]{:S(2)}, u32[]{:S(2)}) %all-to-all-start.2) | async-done | bytes 12582944 | tf_op jit(solution)/shard_map/x_ab1/all_to_all | solution.py:307
  200.6 115.6 %all-to-all-done.1 = bf16[8,2,32,16,768]{4,3,2,1,0:T(8,128)(2,1)} async-done(((bf16[8,2,32,16,768]{4,3,2,1,0:T(8,128)(2,1)}), bf16[8,2,32,16,768]{4,3,2,1,0:T(8,128)(2,1)}, u32[]{:S(2)}, u32[]{:S(2)}) %all-to-all-start.1) | async-done | bytes 12582944 | tf_op jit(solution)/shard_map/x_ab0/all_to_all | solution.py:307
  345.6 113.6 %all-to-all-done = bf16[8,2,32,16,768]{4,3,2,1,0:T(8,128)(2,1)} async-done(((bf16[8,2,32,16,768]{4,3,2,1,0:T(8,128)(2,1)}), bf16[8,2,32,16,768]{4,3,2,1,0:T(8,128)(2,1)}, u32[]{:S(2)}, u32[]{:S(2)}) %all-to-all-start) | async-done | bytes 12582944 | tf_op jit(solution)/shard_map/x_ab2/all_to_all | solution.py:307
  529.7 44.4 %all-to-all-done.6.t_ref = bf16[8,32,16,768]{3,2,1,0:T(8,128)(2,1)} async-done(((bf16[8,32,16,768]{3,2,1,0:T(8,128)(2,1)}), bf16[8,32,16,768]{3,2,1,0:T(8,128)(2,1)}, u32[]{:S(2)}, u32[]{:S(2)}) %all-to-all-start.6) | async-done | bytes 6291488 | tf_op jit(solution)/shard_map/x_t1/all_to_all | solution.py:307
  604.6 44.3 %all-to-all-done.3.t_ref = bf16[8,32,16,768]{3,2,1,0:T(8,128)(2,1)} async-done(((bf16[8,32,16,768]{3,2,1,0:T(8,128)(2,1)}), bf16[8,32,16,768]{3,2,1,0:T(8,128)(2,1)}, u32[]{:S(2)}, u32[]{:S(2)}) %all-to-all-start.3) | async-done | bytes 6291488 | tf_op jit(solution)/shard_map/x_t2/all_to_all | solution.py:307
  654.9 46.7 %pos_b2.1 = (bf16[32,768,128]{2,1,0:T(8,128)(2,1)}, bf16[8,2,32,16,768]{4,3,2,1,0:T(8,128)(2,1)}) custom-call(bf16[96,768,128]{2,1,0:T(8,128)(2,1)} %z_ref.23, bf16[8,32,16,768]{3,2,1,0:T(8,128)(2,1)} %all-to-all-done.3.t_ref, s32[96,1,768]{2,1,0:T(1,128)} %reshape.116.m_ref, f32[2,128]{1,0:T(2,128)} %get-tuple-element.161.lnp_ref, ...), custom_call_target="tpu_custom_call" | custom-call | flops 4831838208 | bytes 60000000 | tf_op jit(solution)/shard_map/pos_b2/pallas_call | solution.py:227
  728.2 46.7 %pos_b0.1 = (bf16[32,768,128]{2,1,0:T(8,128)(2,1)}, bf16[8,2,32,16,768]{4,3,2,1,0:T(8,128)(2,1)}) custom-call(bf16[96,768,128]{2,1,0:T(8,128)(2,1)} %z_ref.23, bf16[8,32,16,768]{3,2,1,0:T(8,128)(2,1)} %all-to-all-done.4.t_ref, s32[96,1,768]{2,1,0:T(1,128)} %reshape.116.m_ref, f32[2,128]{1,0:T(2,128)} %get-tuple-element.161.lnp_ref, ...), custom_call_target="tpu_custom_call" | custom-call | flops 4831838208 | bytes 60000000 | tf_op jit(solution)/shard_map/pos_b0/pallas_call | solution.py:227
  774.9 92.3 %all-to-all-done.8 = bf16[8,2,32,16,768]{4,3,2,1,0:T(8,128)(2,1)} async-done(((bf16[8,2,32,16,768]{4,3,2,1,0:T(8,128)(2,1)}), bf16[8,2,32,16,768]{4,3,2,1,0:T(8,128)(2,1)}, u32[]{:S(2)}, u32[]{:S(2)}) %all-to-all-start.8) | async-done | bytes 12582944 | tf_op jit(solution)/shard_map/x_ab22/all_to_all | solution.py:307
  871.4 46.8 %pos_b1.1 = (bf16[32,768,128]{2,1,0:T(8,128)(2,1)}, bf16[8,2,32,16,768]{4,3,2,1,0:T(8,128)(2,1)}) custom-call(bf16[96,768,128]{2,1,0:T(8,128)(2,1)} %z_ref.23, bf16[8,32,16,768]{3,2,1,0:T(8,128)(2,1)} %all-to-all-done.6.t_ref, s32[96,1,768]{2,1,0:T(1,128)} %reshape.116.m_ref, f32[2,128]{1,0:T(2,128)} %get-tuple-element.161.lnp_ref, ...), custom_call_target="tpu_custom_call" | custom-call | flops 4831838208 | bytes 60000000 | tf_op jit(solution)/shard_map/pos_b1/pallas_call | solution.py:227
  918.2 92.2 %all-to-all-done.5 = bf16[8,2,32,16,768]{4,3,2,1,0:T(8,128)(2,1)} async-done(((bf16[8,2,32,16,768]{4,3,2,1,0:T(8,128)(2,1)}), bf16[8,2,32,16,768]{4,3,2,1,0:T(8,128)(2,1)}, u32[]{:S(2)}, u32[]{:S(2)}) %all-to-all-start.5) | async-done | bytes 12582944 | tf_op jit(solution)/shard_map/x_ab20/all_to_all | solution.py:307
  1039.9 113.6 %all-to-all-done.7 = bf16[8,2,32,16,768]{4,3,2,1,0:T(8,128)(2,1)} async-done(((bf16[8,2,32,16,768]{4,3,2,1,0:T(8,128)(2,1)}), bf16[8,2,32,16,768]{4,3,2,1,0:T(8,128)(2,1)}, u32[]{:S(2)}, u32[]{:S(2)}) %all-to-all-start.7) | async-done | bytes 12582944 | tf_op jit(solution)/shard_map/x_ab21/all_to_all | solution.py:307
  1215.8 62.5 %all-to-all-done.9.t_ref = bf16[8,32,16,768]{3,2,1,0:T(8,128)(2,1)} async-done(((bf16[8,32,16,768]{3,2,1,0:T(8,128)(2,1)}), bf16[8,32,16,768]{3,2,1,0:T(8,128)(2,1)}, u32[]{:S(2)}, u32[]{:S(2)}) %all-to-all-start.9) | async-done | bytes 6291488 | tf_op jit(solution)/shard_map/x_t22/all_to_all | solution.py:307
  1290.8 62.5 %all-to-all-done.11.t_ref = bf16[8,32,16,768]{3,2,1,0:T(8,128)(2,1)} async-done(((bf16[8,32,16,768]{3,2,1,0:T(8,128)(2,1)}), bf16[8,32,16,768]{3,2,1,0:T(8,128)(2,1)}, u32[]{:S(2)}, u32[]{:S(2)}) %all-to-all-start.11) | async-done | bytes 6291488 | tf_op jit(solution)/shard_map/x_t20/all_to_all | solution.py:307
  1357.6 41.4 %pos_c0.1 = (bf16[96,768,128]{2,1,0:T(8,128)(2,1)}, bf16[8,32,16,768]{3,2,1,0:T(8,128)(2,1)}, bf16[32,768,128]{2,1,0:T(8,128)(2,1)}, f32[128,128]{1,0:T(8,128)},...) custom-call(bf16[32,768,128]{2,1,0:T(8,128)(2,1)} %get-tuple-element.77.z_ref.zm_ref, ...), custom_call_target="tpu_custom_call" | custom-call | flops 4831838208 | bytes 60000000 | tf_op jit(solution)/shard_map/pos_c0/pallas_call | solution.py:227
  1431.8 41.6 %pos_c1.1 = (bf16[96,768,128]{2,1,0:T(8,128)(2,1)}, bf16[8,32,16,768]{3,2,1,0:T(8,128)(2,1)}, bf16[32,768,128]{2,1,0:T(8,128)(2,1)}, f32[128,128]{1,0:T(8,128)},...) custom-call(bf16[32,768,128]{2,1,0:T(8,128)(2,1)} %get-tuple-element.75.z_ref.zm_ref, ...), custom_call_target="tpu_custom_call", output_to_operand_aliasing={{0}: (7, {})} | custom-call | flops 4831838208 | bytes 60000000 | tf_op jit(solution)/shard_map/pos_c1/pallas_call | solution.py:227
  1506.8 41.6 %pos_c2.1 = (bf16[96,768,128]{2,1,0:T(8,128)(2,1)}, bf16[8,32,16,768]{3,2,1,0:T(8,128)(2,1)}, bf16[32,768,128]{2,1,0:T(8,128)(2,1)}, f32[128,128]{1,0:T(8,128)},...) custom-call(bf16[32,768,128]{2,1,0:T(8,128)(2,1)} %get-tuple-element.70.z_ref.zm_ref, ...), custom_call_target="tpu_custom_call", output_to_operand_aliasing={{0}: (7, {})} | custom-call | flops 4831838208 | bytes 60000000 | tf_op jit(solution)/shard_map/pos_c2/pallas_call | solution.py:227
  1597.1 56.3 %all-to-all-done.14 = bf16[8,32,16,768]{3,2,1,0:T(8,128)(2,1)} async-done(((bf16[8,32,16,768]{3,2,1,0:T(8,128)(2,1)}), bf16[8,32,16,768]{3,2,1,0:T(8,128)(2,1)}, u32[]{:S(2)}, u32[]{:S(2)}) %all-to-all-start.14) | async-done | bytes 6291488 | tf_op jit(solution)/shard_map/x_dt22/all_to_all | solution.py:307
  1739.7 101.7 %all-to-all-done.18.dab_ref = bf16[8,2,32,16,768]{4,3,2,1,0:T(8,128)(2,1)} async-done(((bf16[8,2,32,16,768]{4,3,2,1,0:T(8,128)(2,1)}), bf16[8,2,32,16,768]{4,3,2,1,0:T(8,128)(2,1)}, u32[]{:S(2)}, u32[]{:S(2)}) %all-to-all-start.18) | async-done | bytes 12582944 | tf_op jit(solution)/shard_map/x_dab20/all_to_all | solution.py:307
  1883.1 101.6 %all-to-all-done.15.dab_ref = bf16[8,2,32,16,768]{4,3,2,1,0:T(8,128)(2,1)} async-done(((bf16[8,2,32,16,768]{4,3,2,1,0:T(8,128)(2,1)}), bf16[8,2,32,16,768]{4,3,2,1,0:T(8,128)(2,1)}, u32[]{:S(2)}, u32[]{:S(2)}) %all-to-all-start.15) | async-done | bytes 12582944 | tf_op jit(solution)/shard_map/x_dab22/all_to_all | solution.py:307
  1988.7 87.0 %pos_d0.1 = (bf16[32,768,128]{2,1,0:T(8,128)(2,1)}, bf16[8,32,16,768]{3,2,1,0:T(8,128)(2,1)}, bf16[32,768,128]{2,1,0:T(8,128)(2,1)}, f32[512,128]{1,0:T(8,128)},...) custom-call(bf16[32,768,128]{2,1,0:T(8,128)(2,1)} %get-tuple-element.77.z_ref.zm_ref, ...), custom_call_target="tpu_custom_call" | custom-call | flops 14495514624 | bytes 60000000 | tf_op jit(solution)/shard_map/pos_d0/pallas_call | solution.py:227
  2075.7 52.0 %all-to-all-done.20.dab_ref = bf16[8,2,32,16,768]{4,3,2,1,0:T(8,128)(2,1)} async-done(((bf16[8,2,32,16,768]{4,3,2,1,0:T(8,128)(2,1)}), bf16[8,2,32,16,768]{4,3,2,1,0:T(8,128)(2,1)}, u32[]{:S(2)}, u32[]{:S(2)}) %all-to-all-start.20) | async-done | bytes 12582944 | tf_op jit(solution)/shard_map/x_dab21/all_to_all | solution.py:307
  2131.2 87.1 %pos_d1.1 = (bf16[32,768,128]{2,1,0:T(8,128)(2,1)}, bf16[8,32,16,768]{3,2,1,0:T(8,128)(2,1)}, bf16[32,768,128]{2,1,0:T(8,128)(2,1)}, f32[512,128]{1,0:T(8,128)},...) custom-call(bf16[32,768,128]{2,1,0:T(8,128)(2,1)} %get-tuple-element.75.z_ref.zm_ref, ...), custom_call_target="tpu_custom_call" | custom-call | flops 14495514624 | bytes 60000000 | tf_op jit(solution)/shard_map/pos_d1/pallas_call | solution.py:227
  2221.9 87.1 %pos_d2.1 = (bf16[32,768,128]{2,1,0:T(8,128)(2,1)}, bf16[8,32,16,768]{3,2,1,0:T(8,128)(2,1)}, bf16[32,768,128]{2,1,0:T(8,128)(2,1)}, f32[512,128]{1,0:T(8,128)},...) custom-call(bf16[32,768,128]{2,1,0:T(8,128)(2,1)} %get-tuple-element.70.z_ref.zm_ref, ...), custom_call_target="tpu_custom_call" | custom-call | flops 14495514624 | bytes 60000000 | tf_op jit(solution)/shard_map/pos_d2/pallas_call | solution.py:227
  2347.5 36.9 %all-to-all-done.16 = bf16[8,32,16,768]{3,2,1,0:T(8,128)(2,1)} async-done(((bf16[8,32,16,768]{3,2,1,0:T(8,128)(2,1)}), bf16[8,32,16,768]{3,2,1,0:T(8,128)(2,1)}, u32[]{:S(2)}, u32[]{:S(2)}) %all-to-all-start.16) | async-done | bytes 6291488 | tf_op jit(solution)/shard_map/x_dt2/all_to_all | solution.py:307
  2422.3 37.1 %all-to-all-done.23.da_ref = bf16[8,32,16,768]{3,2,1,0:T(8,128)(2,1)} async-done(((bf16[8,32,16,768]{3,2,1,0:T(8,128)(2,1)}), bf16[8,32,16,768]{3,2,1,0:T(8,128)(2,1)}, u32[]{:S(2)}, u32[]{:S(2)}) %all-to-all-start.23) | async-done | bytes 6291488 | tf_op jit(solution)/shard_map/x_da1/all_to_all | solution.py:307
  2497.6 37.0 %all-to-all-done.17.da_ref = bf16[8,32,16,768]{3,2,1,0:T(8,128)(2,1)} async-done(((bf16[8,32,16,768]{3,2,1,0:T(8,128)(2,1)}), bf16[8,32,16,768]{3,2,1,0:T(8,128)(2,1)}, u32[]{:S(2)}, u32[]{:S(2)}) %all-to-all-start.17) | async-done | bytes 6291488 | tf_op jit(solution)/shard_map/x_da2/all_to_all | solution.py:307
  2574.9 34.6 %all-to-all-done.25.da_ref = bf16[8,32,16,768]{3,2,1,0:T(8,128)(2,1)} async-done(((bf16[8,32,16,768]{3,2,1,0:T(8,128)(2,1)}), bf16[8,32,16,768]{3,2,1,0:T(8,128)(2,1)}, u32[]{:S(2)}, u32[]{:S(2)}) %all-to-all-start.25) | async-done | bytes 6291488 | tf_op jit(solution)/shard_map/x_da0/all_to_all | solution.py:307
  2622.2 62.5 %all-to-all-done.24.db_ref = bf16[8,32,16,768]{3,2,1,0:T(8,128)(2,1)} async-done(((bf16[8,32,16,768]{3,2,1,0:T(8,128)(2,1)}), bf16[8,32,16,768]{3,2,1,0:T(8,128)(2,1)}, u32[]{:S(2)}, u32[]{:S(2)}) %all-to-all-start.24) | async-done | bytes 6291488 | tf_op jit(solution)/shard_map/x_db1/all_to_all | solution.py:307
  2697.2 62.5 %all-to-all-done.26.db_ref = bf16[8,32,16,768]{3,2,1,0:T(8,128)(2,1)} async-done(((bf16[8,32,16,768]{3,2,1,0:T(8,128)(2,1)}), bf16[8,32,16,768]{3,2,1,0:T(8,128)(2,1)}, u32[]{:S(2)}, u32[]{:S(2)}) %all-to-all-start.26) | async-done | bytes 6291488 | tf_op jit(solution)/shard_map/x_db0/all_to_all | solution.py:307
  2764.6 54.1 %pos_e0.1 = (bf16[96,768,128]{2,1,0:T(8,128)(2,1)}, f32[512,128]{1,0:T(8,128)}, f32[2,8,128]{2,1,0:T(8,128)}) custom-call(bf16[96,768,128]{2,1,0:T(8,128)(2,1)} %z_ref.23, bf16[8,32,16,768]{3,2,1,0:T(8,128)(2,1)} %all-to-all-done.25.da_ref, bf16[8,32,16,768]{3,2,1,0:T(8,128)(2,1)} %all-to-all-done.26.db_ref, bf16[32,768,128]{2,1,0:T(8,128)(2,1)} %get-tuple-element.98.dg_ref, ...), custom_call_target="tpu_custom_call" | custom-call | flops 10468982784 | bytes 60000000 | tf_op jit(solution)/shard_map/pos_e0/pallas_call | solution.py:227
  2818.7 54.2 %pos_e1.1 = (bf16[96,768,128]{2,1,0:T(8,128)(2,1)}, f32[512,128]{1,0:T(8,128)}, f32[2,8,128]{2,1,0:T(8,128)}) custom-call(bf16[96,768,128]{2,1,0:T(8,128)(2,1)} %z_ref.23, bf16[8,32,16,768]{3,2,1,0:T(8,128)(2,1)} %all-to-all-done.23.da_ref, bf16[8,32,16,768]{3,2,1,0:T(8,128)(2,1)} %all-to-all-done.24.db_ref, ...), custom_call_target="tpu_custom_call", output_to_operand_aliasing={{0}: (9, {})} | custom-call | flops 10468982784 | bytes 60000000 | tf_op jit(solution)/shard_map/pos_e1/pallas_call | solution.py:227
  2872.9 54.2 %pos_e2.1 = (bf16[96,768,128]{2,1,0:T(8,128)(2,1)}, f32[512,128]{1,0:T(8,128)}, f32[2,8,128]{2,1,0:T(8,128)}) custom-call(bf16[96,768,128]{2,1,0:T(8,128)(2,1)} %z_ref.23, bf16[8,32,16,768]{3,2,1,0:T(8,128)(2,1)} %all-to-all-done.17.da_ref, bf16[8,32,16,768]{3,2,1,0:T(8,128)(2,1)} %all-to-all-done.22.db_ref, ...), custom_call_target="tpu_custom_call", output_to_operand_aliasing={{0}: (9, {})} | custom-call | flops 10468982784 | bytes 60000000 | tf_op jit(solution)/shard_map/pos_e2/pallas_call | solution.py:227
  (163 shorter events, 832.6 us)
Async XLA Ops:
  28.9 144.2 %all-to-all-start.2 = ((bf16[8,2,32,16,768]{4,3,2,1,0:T(8,128)(2,1)}), bf16[8,2,32,16,768]{4,3,2,1,0:T(8,128)(2,1)}, u32[]{:S(2)}, u32[]{:S(2)}) async-start(bf16[8,2,32,16,768]{4,3,2,1,0:T(8,128)(2,1)} %pos_a1.1), calls=%async_computation.2 | async-start | bytes 25165824 | tf_op jit(solution)/shard_map/x_ab1/all_to_all | solution.py:307
  173.1 143.1 %all-to-all-start.1 = ((bf16[8,2,32,16,768]{4,3,2,1,0:T(8,128)(2,1)}), bf16[8,2,32,16,768]{4,3,2,1,0:T(8,128)(2,1)}, u32[]{:S(2)}, u32[]{:S(2)}) async-start(bf16[8,2,32,16,768]{4,3,2,1,0:T(8,128)(2,1)} %pos_a0.1), calls=%async_computation.1 | async-start | bytes 25165824 | tf_op jit(solution)/shard_map/x_ab0/all_to_all | solution.py:307
  316.2 143.0 %all-to-all-start = ((bf16[8,2,32,16,768]{4,3,2,1,0:T(8,128)(2,1)}), bf16[8,2,32,16,768]{4,3,2,1,0:T(8,128)(2,1)}, u32[]{:S(2)}, u32[]{:S(2)}) async-start(bf16[8,2,32,16,768]{4,3,2,1,0:T(8,128)(2,1)} %pos_a2.1), calls=%async_computation | async-start | bytes 25165824 | tf_op jit(solution)/shard_map/x_ab2/all_to_all | solution.py:307
  498.8 75.2 %all-to-all-start.6 = ((bf16[8,32,16,768]{3,2,1,0:T(8,128)(2,1)}), bf16[8,32,16,768]{3,2,1,0:T(8,128)(2,1)}, u32[]{:S(2)}, u32[]{:S(2)}) async-start(bf16[8,32,16,768]{3,2,1,0:T(8,128)(2,1)} %bitcast.185), calls=%async_computation.6 | async-start | bytes 12582912 | tf_op jit(solution)/shard_map/x_t1/all_to_all | solution.py:307
  574.0 75.0 %all-to-all-start.3 = ((bf16[8,32,16,768]{3,2,1,0:T(8,128)(2,1)}), bf16[8,32,16,768]{3,2,1,0:T(8,128)(2,1)}, u32[]{:S(2)}, u32[]{:S(2)}) async-start(bf16[8,32,16,768]{3,2,1,0:T(8,128)(2,1)} %bitcast.181), calls=%async_computation.3 | async-start | bytes 12582912 | tf_op jit(solution)/shard_map/x_t2/all_to_all | solution.py:307
  649.0 75.1 %all-to-all-start.4 = ((bf16[8,32,16,768]{3,2,1,0:T(8,128)(2,1)}), bf16[8,32,16,768]{3,2,1,0:T(8,128)(2,1)}, u32[]{:S(2)}, u32[]{:S(2)}) async-start(bf16[8,32,16,768]{3,2,1,0:T(8,128)(2,1)} %bitcast.176), calls=%async_computation.4 | async-start | bytes 12582912 | tf_op jit(solution)/shard_map/x_t0/all_to_all | solution.py:307
  724.1 143.0 %all-to-all-start.8 = ((bf16[8,2,32,16,768]{4,3,2,1,0:T(8,128)(2,1)}), bf16[8,2,32,16,768]{4,3,2,1,0:T(8,128)(2,1)}, u32[]{:S(2)}, u32[]{:S(2)}) async-start(bf16[8,2,32,16,768]{4,3,2,1,0:T(8,128)(2,1)} %get-tuple-element.73), calls=%async_computation.8 | async-start | bytes 25165824 | tf_op jit(solution)/shard_map/x_ab22/all_to_all | solution.py:307
  867.2 143.3 %all-to-all-start.5 = ((bf16[8,2,32,16,768]{4,3,2,1,0:T(8,128)(2,1)}), bf16[8,2,32,16,768]{4,3,2,1,0:T(8,128)(2,1)}, u32[]{:S(2)}, u32[]{:S(2)}) async-start(bf16[8,2,32,16,768]{4,3,2,1,0:T(8,128)(2,1)} %get-tuple-element.71), calls=%async_computation.5 | async-start | bytes 25165824 | tf_op jit(solution)/shard_map/x_ab20/all_to_all | solution.py:307
  1010.4 143.0 %all-to-all-start.7 = ((bf16[8,2,32,16,768]{4,3,2,1,0:T(8,128)(2,1)}), bf16[8,2,32,16,768]{4,3,2,1,0:T(8,128)(2,1)}, u32[]{:S(2)}, u32[]{:S(2)}) async-start(bf16[8,2,32,16,768]{4,3,2,1,0:T(8,128)(2,1)} %get-tuple-element.72), calls=%async_computation.7 | async-start | bytes 25165824 | tf_op jit(solution)/shard_map/x_ab21/all_to_all | solution.py:307
  1202.9 75.4 %all-to-all-start.9 = ((bf16[8,32,16,768]{3,2,1,0:T(8,128)(2,1)}), bf16[8,32,16,768]{3,2,1,0:T(8,128)(2,1)}, u32[]{:S(2)}, u32[]{:S(2)}) async-start(bf16[8,32,16,768]{3,2,1,0:T(8,128)(2,1)} %bitcast.186), calls=%async_computation.9 | async-start | bytes 12582912 | tf_op jit(solution)/shard_map/x_t22/all_to_all | solution.py:307
  1278.3 75.0 %all-to-all-start.11 = ((bf16[8,32,16,768]{3,2,1,0:T(8,128)(2,1)}), bf16[8,32,16,768]{3,2,1,0:T(8,128)(2,1)}, u32[]{:S(2)}, u32[]{:S(2)}) async-start(bf16[8,32,16,768]{3,2,1,0:T(8,128)(2,1)} %bitcast.182), calls=%async_computation.11 | async-start | bytes 12582912 | tf_op jit(solution)/shard_map/x_t20/all_to_all | solution.py:307
  1353.3 75.0 %all-to-all-start.10 = ((bf16[8,32,16,768]{3,2,1,0:T(8,128)(2,1)}), bf16[8,32,16,768]{3,2,1,0:T(8,128)(2,1)}, u32[]{:S(2)}, u32[]{:S(2)}) async-start(bf16[8,32,16,768]{3,2,1,0:T(8,128)(2,1)} %bitcast.177), calls=%async_computation.10 | async-start | bytes 12582912 | tf_op jit(solution)/shard_map/x_t21/all_to_all | solution.py:307
  1428.3 75.0 %all-to-all-start.12 = ((bf16[8,32,16,768]{3,2,1,0:T(8,128)(2,1)}), bf16[8,32,16,768]{3,2,1,0:T(8,128)(2,1)}, u32[]{:S(2)}, u32[]{:S(2)}) async-start(bf16[8,32,16,768]{3,2,1,0:T(8,128)(2,1)} %get-tuple-element.82), calls=%async_computation.12 | async-start | bytes 12582912 | tf_op jit(solution)/shard_map/x_dt20/all_to_all | solution.py:307
  1503.3 75.0 %all-to-all-start.13 = ((bf16[8,32,16,768]{3,2,1,0:T(8,128)(2,1)}), bf16[8,32,16,768]{3,2,1,0:T(8,128)(2,1)}, u32[]{:S(2)}, u32[]{:S(2)}) async-start(bf16[8,32,16,768]{3,2,1,0:T(8,128)(2,1)} %get-tuple-element.83), calls=%async_computation.13 | async-start | bytes 12582912 | tf_op jit(solution)/shard_map/x_dt21/all_to_all | solution.py:307
  1578.3 75.2 %all-to-all-start.14 = ((bf16[8,32,16,768]{3,2,1,0:T(8,128)(2,1)}), bf16[8,32,16,768]{3,2,1,0:T(8,128)(2,1)}, u32[]{:S(2)}, u32[]{:S(2)}) async-start(bf16[8,32,16,768]{3,2,1,0:T(8,128)(2,1)} %get-tuple-element.84), calls=%async_computation.14 | async-start | bytes 12582912 | tf_op jit(solution)/shard_map/x_dt22/all_to_all | solution.py:307
  1698.4 143.0 %all-to-all-start.18 = ((bf16[8,2,32,16,768]{4,3,2,1,0:T(8,128)(2,1)}), bf16[8,2,32,16,768]{4,3,2,1,0:T(8,128)(2,1)}, u32[]{:S(2)}, u32[]{:S(2)}) async-start(bf16[8,2,32,16,768]{4,3,2,1,0:T(8,128)(2,1)} %bitcast.174), calls=%async_computation.18 | async-start | bytes 25165824 | tf_op jit(solution)/shard_map/x_dab20/all_to_all | solution.py:307
  1841.4 143.3 %all-to-all-start.15 = ((bf16[8,2,32,16,768]{4,3,2,1,0:T(8,128)(2,1)}), bf16[8,2,32,16,768]{4,3,2,1,0:T(8,128)(2,1)}, u32[]{:S(2)}, u32[]{:S(2)}) async-start(bf16[8,2,32,16,768]{4,3,2,1,0:T(8,128)(2,1)} %bitcast.173), calls=%async_computation.15 | async-start | bytes 25165824 | tf_op jit(solution)/shard_map/x_dab22/all_to_all | solution.py:307
  1984.7 143.0 %all-to-all-start.20 = ((bf16[8,2,32,16,768]{4,3,2,1,0:T(8,128)(2,1)}), bf16[8,2,32,16,768]{4,3,2,1,0:T(8,128)(2,1)}, u32[]{:S(2)}, u32[]{:S(2)}) async-start(bf16[8,2,32,16,768]{4,3,2,1,0:T(8,128)(2,1)} %bitcast.172), calls=%async_computation.20 | async-start | bytes 25165824 | tf_op jit(solution)/shard_map/x_dab21/all_to_all | solution.py:307
  2127.7 90.6 %all-to-all-start.19 = ((bf16[8,32,16,768]{3,2,1,0:T(8,128)(2,1)}), bf16[8,32,16,768]{3,2,1,0:T(8,128)(2,1)}, u32[]{:S(2)}, u32[]{:S(2)}) async-start(bf16[8,32,16,768]{3,2,1,0:T(8,128)(2,1)} %get-tuple-element.88), calls=%async_computation.19 | async-start | bytes 12582912 | tf_op jit(solution)/shard_map/x_dt0/all_to_all | solution.py:307
  2218.4 90.6 %all-to-all-start.21 = ((bf16[8,32,16,768]{3,2,1,0:T(8,128)(2,1)}), bf16[8,32,16,768]{3,2,1,0:T(8,128)(2,1)}, u32[]{:S(2)}, u32[]{:S(2)}) async-start(bf16[8,32,16,768]{3,2,1,0:T(8,128)(2,1)} %get-tuple-element.90), calls=%async_computation.21 | async-start | bytes 12582912 | tf_op jit(solution)/shard_map/x_dt1/all_to_all | solution.py:307
  2309.0 75.4 %all-to-all-start.16 = ((bf16[8,32,16,768]{3,2,1,0:T(8,128)(2,1)}), bf16[8,32,16,768]{3,2,1,0:T(8,128)(2,1)}, u32[]{:S(2)}, u32[]{:S(2)}) async-start(bf16[8,32,16,768]{3,2,1,0:T(8,128)(2,1)} %get-tuple-element.86), calls=%async_computation.16 | async-start | bytes 12582912 | tf_op jit(solution)/shard_map/x_dt2/all_to_all | solution.py:307
  2384.4 75.0 %all-to-all-start.23 = ((bf16[8,32,16,768]{3,2,1,0:T(8,128)(2,1)}), bf16[8,32,16,768]{3,2,1,0:T(8,128)(2,1)}, u32[]{:S(2)}, u32[]{:S(2)}) async-start(bf16[8,32,16,768]{3,2,1,0:T(8,128)(2,1)} %bitcast.179), calls=%async_computation.23 | async-start | bytes 12582912 | tf_op jit(solution)/shard_map/x_da1/all_to_all | solution.py:307
  2459.4 75.1 %all-to-all-start.17 = ((bf16[8,32,16,768]{3,2,1,0:T(8,128)(2,1)}), bf16[8,32,16,768]{3,2,1,0:T(8,128)(2,1)}, u32[]{:S(2)}, u32[]{:S(2)}) async-start(bf16[8,32,16,768]{3,2,1,0:T(8,128)(2,1)} %bitcast.180), calls=%async_computation.17 | async-start | bytes 12582912 | tf_op jit(solution)/shard_map/x_da2/all_to_all | solution.py:307
  2534.5 75.0 %all-to-all-start.25 = ((bf16[8,32,16,768]{3,2,1,0:T(8,128)(2,1)}), bf16[8,32,16,768]{3,2,1,0:T(8,128)(2,1)}, u32[]{:S(2)}, u32[]{:S(2)}) async-start(bf16[8,32,16,768]{3,2,1,0:T(8,128)(2,1)} %bitcast.178), calls=%async_computation.25 | async-start | bytes 12582912 | tf_op jit(solution)/shard_map/x_da0/all_to_all | solution.py:307
  2609.5 75.2 %all-to-all-start.24 = ((bf16[8,32,16,768]{3,2,1,0:T(8,128)(2,1)}), bf16[8,32,16,768]{3,2,1,0:T(8,128)(2,1)}, u32[]{:S(2)}, u32[]{:S(2)}) async-start(bf16[8,32,16,768]{3,2,1,0:T(8,128)(2,1)} %bitcast.184), calls=%async_computation.24 | async-start | bytes 12582912 | tf_op jit(solution)/shard_map/x_db1/all_to_all | solution.py:307
  2684.7 75.0 %all-to-all-start.26 = ((bf16[8,32,16,768]{3,2,1,0:T(8,128)(2,1)}), bf16[8,32,16,768]{3,2,1,0:T(8,128)(2,1)}, u32[]{:S(2)}, u32[]{:S(2)}) async-start(bf16[8,32,16,768]{3,2,1,0:T(8,128)(2,1)} %bitcast.183), calls=%async_computation.26 | async-start | bytes 12582912 | tf_op jit(solution)/shard_map/x_db0/all_to_all | solution.py:307
  2759.9 4.6 copy-start
  2759.9 112.9 %all-to-all-start.22 = ((bf16[8,32,16,768]{3,2,1,0:T(8,128)(2,1)}), bf16[8,32,16,768]{3,2,1,0:T(8,128)(2,1)}, u32[]{:S(2)}, u32[]{:S(2)}) async-start(bf16[8,32,16,768]{3,2,1,0:T(8,128)(2,1)} %bitcast.175), calls=%async_computation.22 | async-start | bytes 12582912 | tf_op jit(solution)/shard_map/x_db2/all_to_all | solution.py:307
  2872.8 54.2 %copy-start.3 = (f32[512,128]{1,0:T(8,128)S(1)}, f32[512,128]{1,0:T(8,128)}, u32[]{:S(2)}) copy-start(f32[512,128]{1,0:T(8,128)} %get-tuple-element.109) | copy-start | bytes 786436
  2872.9 54.2 %copy-start.4 = (f32[512,128]{1,0:T(8,128)S(1)}, f32[512,128]{1,0:T(8,128)}, u32[]{:S(2)}) copy-start(f32[512,128]{1,0:T(8,128)} %get-tuple-element.110) | copy-start | bytes 786436
  2872.9 55.3 %copy-start.28 = (f32[2,8,128]{2,1,0:T(8,128)S(1)}, f32[2,8,128]{2,1,0:T(8,128)}, u32[]{:S(2)}) copy-start(f32[2,8,128]{2,1,0:T(8,128)} %get-tuple-element.103) | copy-start | bytes 24580
  2872.9 55.3 %copy-start.29 = (f32[2,8,128]{2,1,0:T(8,128)S(1)}, f32[2,8,128]{2,1,0:T(8,128)}, u32[]{:S(2)}) copy-start(f32[2,8,128]{2,1,0:T(8,128)} %get-tuple-element.104) | copy-start | bytes 24580
  (26 other events, 113.9 us)
